TPU v7x, 128 devices: a whole 4x4x4 slice. The times are simulated.
128 devices in a mesh: shard: 16 (over z, y), tp: 8 (over x, core).
Axes of the slice: x: 4, y: 4, z: 4, core: 2. Of those that a mesh axis runs over, the one named last changes fastest.
Arguments:
- train_query: bfloat16 [8192, 8192], P('shard', 'tp'), may hold values from -0.0625 to 0.0625
- low_query: bfloat16 [8192, 16], P('shard'), may hold values from -0.0625 to 0.0625
- high_query: bfloat16 [16, 8192], P(None, 'tp'), may hold values from -1.5 to 1.5
- train_key: bfloat16 [8192, 1024], P('shard', 'tp'), may hold values from -0.0625 to 0.0625
- low_key: bfloat16 [8192, 16], P('shard'), may hold values from -0.0625 to 0.0625
- high_key: bfloat16 [16, 1024], P(None, 'tp'), may hold values from -1.5 to 1.5
- train_value: bfloat16 [8192, 1024], P('shard', 'tp'), may hold values from -0.0625 to 0.0625
- low_value: bfloat16 [8192, 16], P('shard'), may hold values from -0.0625 to 0.0625
- high_value: bfloat16 [16, 1024], P(None, 'tp'), may hold values from -1.5 to 1.5
- norm_train: float32 [8192], P(('shard', 'tp')), may hold values from 0.25 to 1.75
- norm_step: float32 [8192], P(('shard', 'tp')), may hold values from -0.3 to 0.3
Outputs:
- serving_query: bfloat16 [8192, 8192], P('tp')
- serving_key: bfloat16 [1024, 8192], P('tp')
- serving_value: bfloat16 [1024, 8192], P('tp')
- serve_norm: bfloat16 [8192], replicated
All inputs are finite; a program needn't handle non-finite values.
Results may differ from a plain program's by a relative error of at most 0.001.
Values may be sent and summed in bfloat16 or wider, within the bound.
A program may use at most 128 MiB of HBM per device.

v0:
```python
import jax
import jax.numpy as jnp
from jax import lax
from jax.sharding import PartitionSpec as P

mix_rate = 0.5


def side_by_side(arrays, axis, dim, along):
    ends, at = ([], 0)
    for a in arrays[:-1]:
        at += a.shape[along]
        ends.append(at)
    both = jnp.concatenate(arrays, axis=along)
    return tuple(jnp.split(lax.all_gather(both, axis, axis=dim, tiled=True), ends, axis=along))


def per_device(
    train_query,
    low_query,
    high_query,
    train_key,
    low_key,
    high_key,
    train_value,
    low_value,
    high_value,
    norm_train,
    norm_step,
):
    whole_query = train_query.astype(jnp.float32) + mix_rate * jnp.dot(
        low_query, high_query, preferred_element_type=jnp.float32
    )
    whole_key = train_key.astype(jnp.float32) + mix_rate * jnp.dot(
        low_key, high_key, preferred_element_type=jnp.float32
    )
    whole_value = train_value.astype(jnp.float32) + mix_rate * jnp.dot(
        low_value, high_value, preferred_element_type=jnp.float32
    )
    narrow_query, narrow_key, narrow_value = (
        whole_query.astype(jnp.bfloat16),
        whole_key.astype(jnp.bfloat16),
        whole_value.astype(jnp.bfloat16),
    )
    serving_query, serving_key, serving_value = side_by_side(
        (narrow_query, narrow_key, narrow_value), "shard", 0, 1
    )
    serving_query, serving_key, serving_value = (serving_query.T, serving_key.T, serving_value.T)
    serve_norm = lax.all_gather(
        (norm_train + norm_step).astype(jnp.bfloat16), ("shard", "tp"), axis=0, tiled=True
    )
    return (serving_query, serving_key, serving_value, serve_norm)


def solution(mesh):
    in_specs = (
        P("shard", "tp"),
        P("shard", None),
        P(None, "tp"),
        P("shard", "tp"),
        P("shard", None),
        P(None, "tp"),
        P("shard", "tp"),
        P("shard", None),
        P(None, "tp"),
        P(("shard", "tp")),
        P(("shard", "tp")),
    )
    out_specs = (P("tp", None), P("tp", None), P("tp", None), P())
    return jax.shard_map(
        per_device, mesh=mesh, in_specs=in_specs, out_specs=out_specs, check_vma=False
    )
```

profile of v0, /device:TPU:0, one launch (start us, length us, event | category | flops | bytes accessed | tf_op | source)
XLA Modules:
  0.0 200.6 jit_solution(366831864264587598)
XLA Ops:
  7.2 0.0 copy-start
  7.2 0.0 copy-start.1
  7.2 0.0 copy-start.3
  7.2 0.0 copy-start.5
  7.2 0.0 copy-start.2
  7.2 0.0 copy-start.4
  7.2 0.0 copy-start.6
  7.2 0.0 all-gather.2.cloned.1.call-start
  7.3 0.6 copy-done
  7.9 1.7 add_convert_fusion
  9.6 0.0 copy-done.1
  9.6 0.0 copy-done.3
  9.7 0.0 copy-done.5
  9.7 0.2 fusion.2
  9.9 0.0 copy-done.2
  9.9 0.0 copy-done.4
  9.9 0.0 copy-done.6
  9.9 0.0 copy-start.7
  9.9 0.0 copy-start.8
  10.0 0.2 fusion.3
  10.2 1.2 pad_maximum_fusion
  11.3 0.0 all-gather.2.cloned.1.call-update
  11.4 0.0 copy-done.7
  11.4 0.0 copy-done.8
  11.4 0.2 dynamic-update-slice
  11.7 71.5 %all-reduce = bf16[8192]{0:T(1024)(128)(2,1)} all-reduce(bf16[8192]{0:T(1024)(128)(2,1)S(1)} %dynamic-update-slice), channel_id=1, replica_groups=mesh['shard'=16,'tp'=8] {'shard','tp'}, use_global_device_ids=true, to_apply=%add | all-reduce | flops 8192 | bytes 32768
  83.2 64.6 %all-gather.2.cloned.1.call-done = bf16[8192,1280]{1,0:T(8,128)(2,1)} async-done(((bf16[512,1280]{1,0:T(8,128)(2,1)}), bf16[8192,1280]{1,0:T(8,128)(2,1)}) %all-gather.2.cloned.1.call-update) | async-done | bytes 20971536 | tf_op jit(solution)/shard_map/all_gather | solution.py:15
  147.8 3.8 %slice_bitcast_fusion.1 = (bf16[128,8192]{0,1:T(8,128)(2,1)S(1)}, bf16[128,8192]{0,1:T(8,128)(2,1)}) fusion(bf16[8192,1280]{1,0:T(8,128)(2,1)} %all-gather.2.cloned.1.call-done), kind=kLoop, calls=%fused_computation.1 | loop fusion | bytes 8388608 | tf_op jit(solution)/shard_map/transpose | solution.py:48
  151.6 4.1 %copy.18 = bf16[128,8192]{1,0:T(8,128)(2,1)} copy(bf16[128,8192]{0,1:T(8,128)(2,1)} %get-tuple-element.9) | data formatting | bytes 4194304
  155.7 2.9 %copy.19 = bf16[128,8192]{1,0:T(8,128)(2,1)} copy(bf16[128,8192]{0,1:T(8,128)(2,1)S(1)} %get-tuple-element.8) | data formatting | bytes 4194304
  158.6 14.0 %slice_bitcast_fusion = bf16[1024,8192]{0,1:T(8,128)(2,1)} fusion(bf16[8192,1280]{1,0:T(8,128)(2,1)} %all-gather.2.cloned.1.call-done), kind=kLoop, calls=%fused_computation | loop fusion | bytes 33554432 | tf_op jit(solution)/shard_map/transpose | solution.py:48
  172.5 21.2 %copy.17 = bf16[1024,8192]{1,0:T(8,128)(2,1)} copy(bf16[1024,8192]{0,1:T(8,128)(2,1)} %slice_bitcast_fusion) | data formatting | bytes 33554432
  (2 shorter events, 0.0 us)
Async XLA Ops:
  7.2 0.8 copy-start
  7.2 2.5 %copy-start.1 = (bf16[512,128]{1,0:T(8,128)(2,1)S(1)}, bf16[512,128]{1,0:T(8,128)(2,1)}, u32[]{:S(2)}) copy-start(bf16[512,128]{1,0:T(8,128)(2,1)} %param.14) | copy-start | bytes 393220
  7.2 2.5 %copy-start.3 = (bf16[512,16]{0,1:T(8,128)(2,1)S(1)}, bf16[512,16]{0,1:T(8,128)(2,1)}, u32[]{:S(2)}) copy-start(bf16[512,16]{0,1:T(8,128)(2,1)} %param.15) | copy-start | bytes 49156
  7.2 2.5 %copy-start.5 = (bf16[16,128]{1,0:T(8,128)(2,1)S(1)}, bf16[16,128]{1,0:T(8,128)(2,1)}, u32[]{:S(2)}) copy-start(bf16[16,128]{1,0:T(8,128)(2,1)} %param.16) | copy-start | bytes 12292
  7.2 2.7 %copy-start.2 = (bf16[512,128]{1,0:T(8,128)(2,1)S(1)}, bf16[512,128]{1,0:T(8,128)(2,1)}, u32[]{:S(2)}) copy-start(bf16[512,128]{1,0:T(8,128)(2,1)} %param.17) | copy-start | bytes 393220
  7.2 2.7 %copy-start.4 = (bf16[512,16]{0,1:T(8,128)(2,1)S(1)}, bf16[512,16]{0,1:T(8,128)(2,1)}, u32[]{:S(2)}) copy-start(bf16[512,16]{0,1:T(8,128)(2,1)} %param.18) | copy-start | bytes 49156
  7.2 2.7 %copy-start.6 = (bf16[16,128]{1,0:T(8,128)(2,1)S(1)}, bf16[16,128]{1,0:T(8,128)(2,1)}, u32[]{:S(2)}) copy-start(bf16[16,128]{1,0:T(8,128)(2,1)} %param.19) | copy-start | bytes 12292
  7.2 140.6 %all-gather.2.cloned.1.call-start = ((), (), s32[]{:S(2)}) async-start(), calls=%async_computation | async-start | bytes 22282240 | tf_op jit(solution)/shard_map/all_gather | solution.py:15
  9.9 1.4 copy-start.7
  9.9 1.4 copy-start.8
Sparse Core Ops, SparseCore 0:
  11.5 136.2 all-gather.1
where the time goes:
time: 202 us; the launch traced here: 201 us
  blocking collectives  71.5 us (35%)
  waiting for transfers between devices  64.6 us (32%)
  local copies, waits for them, and re-layouts  46.9 us (23%)
  between operations  14.2 us (7%)
  matrix products  2.15 us (1%)
    unnamed x1, blocking collectives  71.5 us
    all_gather x1, waiting for transfers between devices, side_by_side(): lax.all_gather(both, axis, axis=dim, tiled=True)  64.6 us
    unnamed x23, local copies, waits for them, and re-layouts  29.1 us
    transpose x2, local copies, waits for them, and re-layouts, per_device(): serving_query, serving_key, serving_value = (serving_query.T, serving_key...  17.8 us
  transfers between devices with their start and end apart: 1, of which 1 were waited for; matrix products, arithmetic and copies ran while one was open for 0% of the time, Pallas kernels for 0%

commit v1 on v0

v1 whole, which is shorter than its diff:
```python
import jax
import jax.numpy as jnp
from jax import lax
from jax.experimental import pallas as pl
from jax.experimental.pallas import tpu as pltpu
from jax.sharding import PartitionSpec as P

MESH = pl.DeviceIdType.MESH
mix_rate = 0.5

ROWS, COLS, TILE = 1280, 512, 128
PART = ROWS // 4
SLOTS = 15
A, B, C, D = 0, 1, 2, 3


def schedule():
    near = (0, -1, 1, 2)
    y_up = [(0, 0, A), (0, 0, B), (-1, 0, A)]
    y_down = [(0, 0, B), (0, 0, A), (1, 0, B)]
    z_up = [(0, 0, C), (0, 0, D), (0, -1, C)]
    z_down = [(0, 0, D), (0, 0, C), (0, 1, D)]
    for far in near:
        z_up += [(far, 0, A), (far, 0, B), (far, -1, A)]
        z_down += [(far, 0, B), (far, 0, A), (far, 1, B)]
        y_up += [(0, far, C), (0, far, D), (-1, far, C)]
        y_down += [(0, far, D), (0, far, C), (1, far, D)]
    return (((1, 0), y_up), ((-1, 0), y_down), ((0, 1), z_up), ((0, -1), z_down))


LINKS = schedule()
TILES = (
    (0, ((0, 0, 128),)),
    (4, ((1, 512, 128),)),
    (5, ((2, 640, 128),)),
    (9, ((3, 1152, 128),)),
    (1, ((0, 128, 128),)),
    (3, ((1, 384, 128),)),
    (6, ((2, 768, 128),)),
    (8, ((3, 1024, 128),)),
    (2, ((0, 256, 64), (1, 320, 64))),
    (7, ((2, 896, 64), (3, 960, 64))),
)


def gather_kernel(
    tq, lq, hq, tk, lk, hk, tv, lv, hv, nt, ns,
    out, norm_out,
    t_in, l_in, h_in, nt_in, ns_in, norm_all, norm_rows,
    load_sem, send_sem, recv_sem, norm_send, norm_recv,
):
    shard, tp = lax.axis_index("shard"), lax.axis_index("tp")
    z, y = shard // 4, shard % 4
    x, core = tp // 2, tp % 2

    def at(dy, dz):
        return ((z + dz + 4) % 4) * 4 + (y + dy + 4) % 4

    def other(dx):
        return ((x + dx + 4) % 4) * 2 + core

    loads = {}

    def load(name, src, dst):
        loads[name] = pltpu.make_async_copy(src, dst, load_sem.at[len(loads)])
        loads[name].start()

    def load_tile(tile):
        if tile < 8:
            load(("t", tile), tq.at[:, pl.ds(tile * TILE, TILE)], t_in.at[tile])
        else:
            load(("t", tile), (tk, tv)[tile - 8], t_in.at[tile])

    load(("l", 0), lq, l_in.at[0])
    load(("h", 0), hq, h_in.at[:, pl.ds(0, 1024)])
    for tile, _ in TILES[:3]:
        load_tile(tile)
    load(("l", 2), lv, l_in.at[2])
    load(("h", 2), hv, h_in.at[:, pl.ds(1152, TILE)])
    for tile, _ in TILES[3:7]:
        load_tile(tile)
    load(("l", 1), lk, l_in.at[1])
    load(("h", 1), hk, h_in.at[:, pl.ds(1024, TILE)])
    for tile, _ in TILES[7:]:
        load_tile(tile)
    load("nt", nt, nt_in)
    load("ns", ns, ns_in)

    barrier = pltpu.get_barrier_semaphore()
    for (dy, dz), _ in LINKS:
        pl.semaphore_signal(barrier, inc=1, device_id={"shard": at(dy, dz)}, device_id_type=MESH)
    for peer in (x * 2 + 1 - core, other(1), other(-1)):
        pl.semaphore_signal(barrier, inc=1, device_id={"tp": peer}, device_id_type=MESH)

    def send(link, slot, rows=None):
        (ty, tz), items = LINKS[link]
        dy, dz, part = items[slot]
        row, count = rows if rows is not None else (part * PART, PART)
        piece = out.at[at(dy, dz), pl.ds(row, count)]
        return pltpu.make_async_remote_copy(
            src_ref=piece, dst_ref=piece, send_sem=send_sem.at[link, slot], recv_sem=recv_sem.at[link, slot],
            device_id={"shard": at(ty, tz)}, device_id_type=MESH,
        )

    def arrival(link, slot):
        (ty, tz), items = LINKS[link]
        dy, dz, part = items[slot]
        piece = out.at[at(dy - ty, dz - tz), pl.ds(part * PART, PART)]
        return pltpu.make_async_remote_copy(
            src_ref=piece, dst_ref=piece, send_sem=send_sem.at[link, slot], recv_sem=recv_sem.at[link, slot],
            device_id={"shard": at(ty, tz)}, device_id_type=MESH,
        )

    def merge(tile):
        loads[("t", tile)].wait()
        which = max(tile - 7, 0)
        for name in (("l", which), ("h", which)):
            if name in loads:
                loads.pop(name).wait()
        product = lax.dot_general(
            h_in[:, tile * TILE:(tile + 1) * TILE], l_in[which], (((0,), (0,)), ((), ())),
            preferred_element_type=jnp.float32,
        )
        whole = t_in[tile].astype(jnp.float32).T + mix_rate * product
        out[shard, tile * TILE:(tile + 1) * TILE, :] = whole.astype(jnp.bfloat16)

    waiting = ()
    for place, (tile, pieces) in enumerate(TILES):
        merge(tile)
        if place == 1:
            pl.semaphore_wait(barrier, 7)
        for link, row, count in waiting:
            send(link, 0, (row, count)).start()
        waiting = pieces
    for link, row, count in waiting:
        send(link, 0, (row, count)).start()
    for link in range(4):
        send(link, 1).start()

    loads["nt"].wait()
    loads["ns"].wait()
    gain = nt_in[...] + ns_in[...]
    both = jnp.concatenate([gain, gain], axis=1)
    half = lax.broadcasted_iota(jnp.int32, (1, 128), 1) // 64
    norm_all[shard, tp] = jnp.where(half == core, both, 0.0)

    def norm_copy(step, piece, peer):
        return pltpu.make_async_remote_copy(
            src_ref=piece, dst_ref=piece, send_sem=norm_send.at[step], recv_sem=norm_recv.at[step],
            device_id=peer, device_id_type=MESH,
        )

    def pair(dx):
        return norm_all.at[shard, pl.ds(((x + dx + 4) % 4) * 2, 2)]

    def row_of(dy):
        return norm_all.at[at(dy, 0)]

    def plane_of(dz):
        return norm_all.at[pl.ds(((z + dz + 4) % 4) * 4, 4)]

    own = norm_all.at[shard, tp]
    twin = norm_all.at[shard, x * 2 + 1 - core]
    norm_steps = (
        ((0, own, {"tp": x * 2 + 1 - core}, twin),),
        ((1, pair(0), {"tp": other(1)}, pair(-1)), (2, pair(0), {"tp": other(-1)}, pair(1))),
        ((3, pair(-1), {"tp": other(1)}, pair(2)),),
        ((4, row_of(0), {"shard": at(1, 0)}, row_of(-1)), (5, row_of(0), {"shard": at(-1, 0)}, row_of(1))),
        ((6, row_of(-1), {"shard": at(1, 0)}, row_of(2)),),
        ((7, plane_of(0), {"shard": at(0, 1)}, plane_of(-1)), (8, plane_of(0), {"shard": at(0, -1)}, plane_of(1))),
        ((9, plane_of(-1), {"shard": at(0, 1)}, plane_of(2)),),
    )

    def norm_start(step):
        for sem, sent, peer, _ in norm_steps[step]:
            norm_copy(sem, sent, peer).start()

    def norm_wait(step):
        for sem, sent, peer, arrived in norm_steps[step]:
            norm_copy(sem, sent, peer).wait_send()
            norm_copy(sem, arrived, peer).wait_recv()

    norm_start(0)
    for slot in range(SLOTS):
        for link in range(4):
            arrival(link, slot).wait_recv()
        if slot < len(norm_steps):
            norm_wait(slot)
        if slot + 1 < len(norm_steps):
            norm_start(slot + 1)
        if slot + 2 < SLOTS:
            for link in range(4):
                send(link, slot + 2).start()
        if slot == len(norm_steps):
            for row in range(64):
                first = norm_all[row // 4, (row % 4) * 2]
                second = norm_all[row // 4, (row % 4) * 2 + 1]
                norm_rows[row:row + 1, :] = first + second
            norm_out[...] = norm_rows[...].astype(jnp.bfloat16)
    for slot in range(SLOTS):
        for link in range(4):
            (_, _), items = LINKS[link]
            send(link, slot).wait_send()


def write_kernel(block, norm, q, k, v, n, sem):
    copies = []

    def copy(src, dst):
        copies.append(pltpu.make_async_copy(src, dst, sem.at[len(copies)]))
        copies[-1].start()

    for s in range(16):
        columns = pl.ds(s * COLS, COLS)
        copy(block.at[s, pl.ds(0, 1024)], q.at[:, columns])
        copy(block.at[s, pl.ds(1024, 128)], k.at[:, columns])
        copy(block.at[s, pl.ds(1152, 128)], v.at[:, columns])
    copy(norm, n)
    for c in copies:
        c.wait()


def per_device(tq, lq, hq, tk, lk, hk, tv, lv, hv, nt, ns):
    hbm = pl.BlockSpec(memory_space=pltpu.HBM)
    vmem = pl.BlockSpec(memory_space=pltpu.VMEM)
    bf16, f32 = jnp.bfloat16, jnp.float32
    block, norm = pl.pallas_call(
        gather_kernel,
        out_shape=(pltpu.VMEM((16, ROWS, COLS), bf16), pltpu.VMEM((64, 128), bf16)),
        in_specs=[hbm] * 11,
        out_specs=(vmem, vmem),
        scratch_shapes=[
            pltpu.VMEM((10, COLS, TILE), bf16),
            pltpu.VMEM((3, 16, COLS), bf16),
            pltpu.VMEM((16, ROWS), bf16),
            pltpu.VMEM((1, 64), f32),
            pltpu.VMEM((1, 64), f32),
            pltpu.VMEM((16, 8, 1, 128), f32),
            pltpu.VMEM((64, 128), f32),
            pltpu.SemaphoreType.DMA((18,)),
            pltpu.SemaphoreType.DMA((4, SLOTS)),
            pltpu.SemaphoreType.DMA((4, SLOTS)),
            pltpu.SemaphoreType.DMA((10,)),
            pltpu.SemaphoreType.DMA((10,)),
        ],
        compiler_params=pltpu.CompilerParams(
            collective_id=0, has_side_effects=True, vmem_limit_bytes=12 * 1024 * 1024
        ),
        name="gather",
    )(*(
        pltpu.with_memory_space_constraint(a, pltpu.HBM)
        for a in (tq, lq.T, hq, tk, lk.T, hk, tv, lv.T, hv, nt.reshape(1, 64), ns.reshape(1, 64))
    ))
    q, k, v, n = pl.pallas_call(
        write_kernel,
        out_shape=(
            jax.ShapeDtypeStruct((1024, 8192), bf16),
            jax.ShapeDtypeStruct((128, 8192), bf16),
            jax.ShapeDtypeStruct((128, 8192), bf16),
            jax.ShapeDtypeStruct((64, 128), bf16),
        ),
        in_specs=[vmem, vmem],
        out_specs=(hbm,) * 4,
        scratch_shapes=[pltpu.SemaphoreType.DMA((49,))],
        compiler_params=pltpu.CompilerParams(vmem_limit_bytes=12 * 1024 * 1024),
        name="write",
    )(block, norm)
    return q, k, v, n.reshape(8192)


def solution(mesh):
    in_specs = (
        P("shard", "tp"), P("shard", None), P(None, "tp"),
        P("shard", "tp"), P("shard", None), P(None, "tp"),
        P("shard", "tp"), P("shard", None), P(None, "tp"),
        P(("shard", "tp")), P(("shard", "tp")),
    )
    out_specs = (P("tp", None), P("tp", None), P("tp", None), P())
    return jax.shard_map(per_device, mesh=mesh, in_specs=in_specs, out_specs=out_specs, check_vma=False)
```

time: 202 us -> 124 us (0.61)
  Pallas kernels: 0 us -> 123 us
  blocking collectives: 71.5 us -> 0 us
  waiting for transfers between devices: 64.6 us -> 0 us
  local copies, waits for them, and re-layouts: 46.9 us -> 0 us
  between operations: 14.2 us -> 0.64 us
  matrix products: 2.15 us -> 0 us
    pallas_call x0 -> x2, Pallas kernels: none -> 123 us  [the longest x1 116 us: per_device(): pl.pallas_call(gather_kernel, out_shape=(pltpu.VMEM((16, ROWS, COLS), bf1...]
    unnamed x1 -> x0, blocking collectives: 71.5 us -> none
    all_gather x1 -> x0, waiting for transfers between devices: 64.6 us -> none  [side_by_side(): lax.all_gather(both, axis, axis=dim, tiled=True)]
    unnamed x23 -> x0, local copies, waits for them, and re-layouts: 29.1 us -> none
    transpose x2 -> x0, local copies, waits for them, and re-layouts: 17.8 us -> none  [per_device(): serving_query, serving_key, serving_value = (serving_query.T, serving_key...]
    dot_general x3 -> x0, matrix products: 2.15 us -> none  [the longest x1 1.7 us: per_device(): jnp.dot(low_query, high_query, preferred_element_type=jnp.float32)]
  transfers between devices with their start and end apart: 1 -> 0, of which waited for: 1 -> 0; matrix products, arithmetic and copies ran while one was open for 0% -> 0% of each run, Pallas kernels for 0% -> 0%
where the time goes in v1:
time: 124 us
  Pallas kernels  123 us (99%)
    pallas_call x1, Pallas kernels, per_device(): pl.pallas_call(gather_kernel, out_shape=(pltpu.VMEM((16, ROWS, COLS), bf1...  116 us
    pallas_call x1, Pallas kernels, per_device(): pl.pallas_call(write_kernel, out_shape=(jax.ShapeDtypeStruct((1024, 8192)...  7.49 us

profile of v1, /device:TPU:0, one launch (start us, length us, event | category | flops | bytes accessed | tf_op | source)
XLA Modules:
  0.0 123.7 jit_solution(7734159361443998932)
XLA Ops:
  0.6 115.6 %gather.1 = (bf16[16,1280,512]{2,1,0:T(8,128)(2,1)S(1)}, bf16[64,128]{1,0:T(8,128)(2,1)S(1)}) custom-call(bf16[512,1024]{1,0:T(8,128)(2,1)} %tq.1, bf16[16,512]{1,0:T(8,128)(2,1)} %bitcast.6, bf16[16,1024]{1,0:T(8,128)(2,1)} %hq.1, bf16[512,128]{1,0:T(8,128)(2,1)} %tk.1, bf16[16,512]{1,0:T(8,128)(2,1)} %bitcast.7, bf16[16,128]{1,0:T(8,128)(2,1)} %hk.1, ...), custom_call_target="tpu_custom_call" | custom-call | tf_op jit(solution)/shard_map/gather/pallas_call | solution.py:227
  116.2 7.5 %write.1 = (bf16[1024,8192]{1,0:T(8,128)(2,1)}, bf16[128,8192]{1,0:T(8,128)(2,1)}, bf16[128,8192]{1,0:T(8,128)(2,1)}, bf16[64,128]{1,0:T(8,128)(2,1)}) custom-call(bf16[16,1280,512]{2,1,0:T(8,128)(2,1)S(1)} %get-tuple-element.10.block, bf16[64,128]{1,0:T(8,128)(2,1)S(1)} %get-tuple-element.11.norm), custom_call_target="tpu_custom_call" | custom-call | tf_op jit(solution)/shard_map/write/pallas_call | solution.py:254

commit v2 on v1

--- a/solution.py
+++ b/solution.py
@@ -15,31 +15,41 @@
 
 
 def schedule():
-    near = (0, -1, 1, 2)
-    y_up = [(0, 0, A), (0, 0, B), (-1, 0, A)]
-    y_down = [(0, 0, B), (0, 0, A), (1, 0, B)]
-    z_up = [(0, 0, C), (0, 0, D), (0, -1, C)]
-    z_down = [(0, 0, D), (0, 0, C), (0, 1, D)]
-    for far in near:
-        z_up += [(far, 0, A), (far, 0, B), (far, -1, A)]
-        z_down += [(far, 0, B), (far, 0, A), (far, 1, B)]
-        y_up += [(0, far, C), (0, far, D), (-1, far, C)]
-        y_down += [(0, far, D), (0, far, C), (1, far, D)]
-    return (((1, 0), y_up), ((-1, 0), y_down), ((0, 1), z_up), ((0, -1), z_down))
-
-
+    def order(first, second, own_first, own_second, step, place):
+        side = lambda far: place(0, far)
+        return [
+            side(0) + (first,), side(0) + (second,), side(0) + (own_first,), side(0) + (own_second,),
+            place(-step, 0) + (first,),
+            side(-1) + (own_first,), side(-1) + (own_second,),
+            place(-step, 0) + (own_first,),
+            side(1) + (own_first,), side(1) + (own_second,),
+            side(2) + (own_first,), side(2) + (own_second,),
+            place(-step, -1) + (own_first,), place(-step, 1) + (own_first,), place(-step, 2) + (own_first,),
+        ]
+
+    along_y = lambda along, across: (along, across)
+    along_z = lambda along, across: (across, along)
+    return (
+        ((1, 0), order(A, B, C, D, 1, along_y)),
+        ((-1, 0), order(B, A, D, C, -1, along_y)),
+        ((0, 1), order(C, D, A, B, 1, along_z)),
+        ((0, -1), order(D, C, B, A, -1, along_z)),
+    )
+
+
+AHEAD = 4
 LINKS = schedule()
 TILES = (
-    (0, ((0, 0, 128),)),
-    (4, ((1, 512, 128),)),
-    (5, ((2, 640, 128),)),
-    (9, ((3, 1152, 128),)),
-    (1, ((0, 128, 128),)),
-    (3, ((1, 384, 128),)),
-    (6, ((2, 768, 128),)),
-    (8, ((3, 1024, 128),)),
-    (2, ((0, 256, 64), (1, 320, 64))),
-    (7, ((2, 896, 64), (3, 960, 64))),
+    (0, ((0, 0, 0, 128), (1, 1, 0, 128))),
+    (5, ((2, 0, 640, 128), (3, 1, 640, 128))),
+    (4, ((1, 0, 512, 128),)),
+    (9, ((3, 0, 1152, 128),)),
+    (1, ((0, 0, 128, 128),)),
+    (6, ((2, 0, 768, 128),)),
+    (3, ((1, 0, 384, 128),)),
+    (8, ((3, 0, 1024, 128),)),
+    (2, ((0, 0, 256, 64), (1, 0, 320, 64), (1, 1, 128, 192))),
+    (7, ((2, 0, 896, 64), (3, 0, 960, 64), (3, 1, 768, 192))),
 )
 
 
@@ -129,13 +139,16 @@
         merge(tile)
         if place == 1:
             pl.semaphore_wait(barrier, 7)
-        for link, row, count in waiting:
-            send(link, 0, (row, count)).start()
+        for link, slot, row, count in waiting:
+            send(link, slot, (row, count)).start()
         waiting = pieces
-    for link, row, count in waiting:
-        send(link, 0, (row, count)).start()
-    for link in range(4):
+    for link, slot, row, count in waiting:
+        send(link, slot, (row, count)).start()
+    for link in (0, 2):
         send(link, 1).start()
+    for slot in range(2, AHEAD):
+        for link in range(4):
+            send(link, slot).start()
 
     loads["nt"].wait()
     loads["ns"].wait()
@@ -188,9 +201,9 @@
             norm_wait(slot)
         if slot + 1 < len(norm_steps):
             norm_start(slot + 1)
-        if slot + 2 < SLOTS:
+        if slot + AHEAD < SLOTS:
             for link in range(4):
-                send(link, slot + 2).start()
+                send(link, slot + AHEAD).start()
         if slot == len(norm_steps):
             for row in range(64):
                 first = norm_all[row // 4, (row % 4) * 2]

time: 124 us -> 124 us (level)
  no operation moved by 1% of the time
where the time goes in v2:
time: 124 us
  Pallas kernels  123 us (99%)
    pallas_call x1, Pallas kernels, per_device(): pl.pallas_call(gather_kernel, out_shape=(pltpu.VMEM((16, ROWS, COLS), bf1...  115 us
    pallas_call x1, Pallas kernels, per_device(): pl.pallas_call(write_kernel, out_shape=(jax.ShapeDtypeStruct((1024, 8192)...  7.49 us

profile of v2, /device:TPU:0, one launch (start us, length us, event | category | flops | bytes accessed | tf_op | source)
XLA Modules:
  0.0 123.5 jit_solution(17552775572265310644)
XLA Ops:
  0.6 115.4 %gather.1 = (bf16[16,1280,512]{2,1,0:T(8,128)(2,1)S(1)}, bf16[64,128]{1,0:T(8,128)(2,1)S(1)}) custom-call(bf16[512,1024]{1,0:T(8,128)(2,1)} %tq.1, bf16[16,512]{1,0:T(8,128)(2,1)} %bitcast.6, bf16[16,1024]{1,0:T(8,128)(2,1)} %hq.1, bf16[512,128]{1,0:T(8,128)(2,1)} %tk.1, bf16[16,512]{1,0:T(8,128)(2,1)} %bitcast.7, bf16[16,128]{1,0:T(8,128)(2,1)} %hk.1, ...), custom_call_target="tpu_custom_call" | custom-call | tf_op jit(solution)/shard_map/gather/pallas_call | solution.py:240
  116.0 7.5 %write.1 = (bf16[1024,8192]{1,0:T(8,128)(2,1)}, bf16[128,8192]{1,0:T(8,128)(2,1)}, bf16[128,8192]{1,0:T(8,128)(2,1)}, bf16[64,128]{1,0:T(8,128)(2,1)}) custom-call(bf16[16,1280,512]{2,1,0:T(8,128)(2,1)S(1)} %get-tuple-element.10.block, bf16[64,128]{1,0:T(8,128)(2,1)S(1)} %get-tuple-element.11.norm), custom_call_target="tpu_custom_call" | custom-call | tf_op jit(solution)/shard_map/write/pallas_call | solution.py:267

commit v3 on v2

--- a/solution.py
+++ b/solution.py
@@ -38,7 +38,13 @@
 
 
 AHEAD = 4
+BREAK = (10, 13)
+LATE = SLOTS - BREAK[0]
 LINKS = schedule()
+ARRIVALS = [
+    [(((dy - ty + 1) % 4) - 1, ((dz - tz + 1) % 4) - 1, part) for dy, dz, part in items] for (ty, tz), items in LINKS
+]
+PLACE = {ARRIVALS[link][slot]: (link, slot) for link in range(4) for slot in range(SLOTS)}
 TILES = (
     (0, ((0, 0, 0, 128), (1, 1, 0, 128))),
     (5, ((2, 0, 640, 128), (3, 1, 640, 128))),
@@ -53,18 +59,25 @@
 )
 
 
+def position():
+    shard, core = lax.axis_index("shard"), lax.axis_index("tp") % 2
+    z, y = shard // 4, shard % 4
+
+    def at(dy, dz):
+        return ((z + dz + 4) % 4) * 4 + (y + dy + 4) % 4
+
+    return shard, core, at
+
+
 def gather_kernel(
     tq, lq, hq, tk, lk, hk, tv, lv, hv, nt, ns,
     out, norm_out,
     t_in, l_in, h_in, nt_in, ns_in, norm_all, norm_rows,
     load_sem, send_sem, recv_sem, norm_send, norm_recv,
 ):
-    shard, tp = lax.axis_index("shard"), lax.axis_index("tp")
-    z, y = shard // 4, shard % 4
-    x, core = tp // 2, tp % 2
-
-    def at(dy, dz):
-        return ((z + dz + 4) % 4) * 4 + (y + dy + 4) % 4
+    shard, core, at = position()
+    tp = lax.axis_index("tp")
+    z, x = shard // 4, tp // 2
 
     def other(dx):
         return ((x + dx + 4) % 4) * 2 + core
@@ -193,44 +206,132 @@
             norm_copy(sem, sent, peer).wait_send()
             norm_copy(sem, arrived, peer).wait_recv()
 
-    norm_start(0)
-    for slot in range(SLOTS):
+    def launch(slot):
+        for link in range(4):
+            send(link, slot).start()
+
+    def receive(slot):
         for link in range(4):
             arrival(link, slot).wait_recv()
+
+    def sent(slots):
+        for slot in slots:
+            for link in range(4):
+                send(link, slot).wait_send()
+
+    norm_start(0)
+    first, last = BREAK
+    for slot in range(first):
+        receive(slot)
         if slot < len(norm_steps):
             norm_wait(slot)
         if slot + 1 < len(norm_steps):
             norm_start(slot + 1)
-        if slot + AHEAD < SLOTS:
-            for link in range(4):
-                send(link, slot + AHEAD).start()
+        if slot + AHEAD < first:
+            launch(slot + AHEAD)
+        elif slot + AHEAD < last:
+            pl.when(core == 1)(lambda: launch(slot + AHEAD))
         if slot == len(norm_steps):
             for row in range(64):
-                first = norm_all[row // 4, (row % 4) * 2]
-                second = norm_all[row // 4, (row % 4) * 2 + 1]
-                norm_rows[row:row + 1, :] = first + second
+                even = norm_all[row // 4, (row % 4) * 2]
+                odd = norm_all[row // 4, (row % 4) * 2 + 1]
+                norm_rows[row:row + 1, :] = even + odd
             norm_out[...] = norm_rows[...].astype(jnp.bfloat16)
-    for slot in range(SLOTS):
-        for link in range(4):
-            (_, _), items = LINKS[link]
-            send(link, slot).wait_send()
+
+    @pl.when(core == 1)
+    def _():
+        for slot in range(first, last):
+            receive(slot)
+            if slot + AHEAD < last:
+                launch(slot + AHEAD)
+        sent(range(first, last))
+
+    sent(range(first))
+
+
+def rest_kernel(block, norm, rest, send_sem, recv_sem):
+    _, core, at = position()
+    barrier = pltpu.get_barrier_semaphore()
+    for (dy, dz), _ in LINKS:
+        pl.semaphore_signal(barrier, inc=1, device_id={"shard": at(dy, dz)}, device_id_type=MESH)
+    pl.semaphore_wait(barrier, 4)
+
+    def run(first):
+        def copy(link, slot):
+            (ty, tz), items = LINKS[link]
+            dy, dz, part = items[slot]
+            from_link, from_slot = PLACE.get(((dy + 1) % 4 - 1, (dz + 1) % 4 - 1, part), (0, -1))
+            if from_slot < first:
+                piece = block.at[at(dy, dz), pl.ds(part * PART, PART)]
+            else:
+                piece = rest.at[from_link, from_slot - first]
+            return pltpu.make_async_remote_copy(
+                src_ref=piece, dst_ref=rest.at[link, slot - first],
+                send_sem=send_sem.at[link, slot - first], recv_sem=recv_sem.at[link, slot - first],
+                device_id={"shard": at(ty, tz)}, device_id_type=MESH,
+            )
+
+        for slot in range(first, min(first + AHEAD, SLOTS)):
+            for link in range(4):
+                copy(link, slot).start()
+        for slot in range(first, SLOTS):
+            for link in range(4):
+                copy(link, slot).wait_recv()
+            if slot + AHEAD < SLOTS:
+                for link in range(4):
+                    copy(link, slot + AHEAD).start()
+        for slot in range(first, SLOTS):
+            for link in range(4):
+                copy(link, slot).wait_send()
+
+    for which in range(2):
+        pl.when(core == which)(lambda: run(BREAK[which]))
+
+
+def write_part(copies, sem, src, owner, part, q, k, v):
+    columns = pl.ds(pl.multiple_of(owner * COLS, COLS), COLS)
+    row, count = part * PART, min(PART, 1024 - part * PART)
+    pieces = [(0, count, q.at[pl.ds(row, count), columns])]
+    if part == D:
+        pieces += [(64, 128, k.at[:, columns]), (192, 128, v.at[:, columns])]
+    for start, rows, dst in pieces:
+        copies.append(pltpu.make_async_copy(src.at[pl.ds(start, rows)], dst, sem.at[len(copies)]))
+        copies[-1].start()
 
 
 def write_kernel(block, norm, q, k, v, n, sem):
-    copies = []
-
-    def copy(src, dst):
-        copies.append(pltpu.make_async_copy(src, dst, sem.at[len(copies)]))
+    shard, core, at = position()
+
+    def run(first):
+        copies = []
+        for part in range(4):
+            for far in range(16):
+                dy, dz = far % 4 - 1, far // 4 - 1
+                if PLACE.get((dy, dz, part), (0, -1))[1] < first:
+                    src = block.at[at(dy, dz), pl.ds(part * PART, PART)]
+                    write_part(copies, sem, src, at(dy, dz), part, q, k, v)
+        copies.append(pltpu.make_async_copy(norm, n, sem.at[len(copies)]))
         copies[-1].start()
-
-    for s in range(16):
-        columns = pl.ds(s * COLS, COLS)
-        copy(block.at[s, pl.ds(0, 1024)], q.at[:, columns])
-        copy(block.at[s, pl.ds(1024, 128)], k.at[:, columns])
-        copy(block.at[s, pl.ds(1152, 128)], v.at[:, columns])
-    copy(norm, n)
-    for c in copies:
-        c.wait()
+        for c in copies:
+            c.wait()
+
+    for which in range(2):
+        pl.when(core == which)(lambda: run(BREAK[which]))
+
+
+def write_rest_kernel(rest, q_in, k_in, v_in, q, k, v, sem):
+    _, core, at = position()
+
+    def run(first):
+        copies = []
+        for (dy, dz, part), (link, slot) in PLACE.items():
+            if slot >= first:
+                write_part(copies, sem, rest.at[link, slot - first], at(dy, dz), part, q, k, v)
+        for c in copies:
+            c.wait()
+
+    for which in range(2):
+        pl.when(core == which)(lambda: run(BREAK[which]))
 
 
 def per_device(tq, lq, hq, tk, lk, hk, tv, lv, hv, nt, ns):
@@ -264,20 +365,41 @@
         pltpu.with_memory_space_constraint(a, pltpu.HBM)
         for a in (tq, lq.T, hq, tk, lk.T, hk, tv, lv.T, hv, nt.reshape(1, 64), ns.reshape(1, 64))
     ))
+    results = (
+        jax.ShapeDtypeStruct((1024, 8192), bf16),
+        jax.ShapeDtypeStruct((128, 8192), bf16),
+        jax.ShapeDtypeStruct((128, 8192), bf16),
+    )
     q, k, v, n = pl.pallas_call(
         write_kernel,
-        out_shape=(
-            jax.ShapeDtypeStruct((1024, 8192), bf16),
-            jax.ShapeDtypeStruct((128, 8192), bf16),
-            jax.ShapeDtypeStruct((128, 8192), bf16),
-            jax.ShapeDtypeStruct((64, 128), bf16),
-        ),
+        out_shape=results + (jax.ShapeDtypeStruct((64, 128), bf16),),
         in_specs=[vmem, vmem],
         out_specs=(hbm,) * 4,
-        scratch_shapes=[pltpu.SemaphoreType.DMA((49,))],
-        compiler_params=pltpu.CompilerParams(vmem_limit_bytes=12 * 1024 * 1024),
+        scratch_shapes=[pltpu.SemaphoreType.DMA((100,))],
+        compiler_params=pltpu.CompilerParams(vmem_limit_bytes=4 * 1024 * 1024),
         name="write",
     )(block, norm)
+    rest = pl.pallas_call(
+        rest_kernel,
+        out_shape=pltpu.VMEM((4, LATE, PART, COLS), bf16),
+        in_specs=[vmem, hbm],
+        out_specs=vmem,
+        scratch_shapes=[pltpu.SemaphoreType.DMA((4, LATE)), pltpu.SemaphoreType.DMA((4, LATE))],
+        compiler_params=pltpu.CompilerParams(
+            collective_id=1, has_side_effects=True, vmem_limit_bytes=4 * 1024 * 1024
+        ),
+        name="rest",
+    )(block, pltpu.with_memory_space_constraint(n, pltpu.HBM))
+    q, k, v = pl.pallas_call(
+        write_rest_kernel,
+        out_shape=results,
+        in_specs=[vmem] + [hbm] * 3,
+        out_specs=(hbm,) * 3,
+        input_output_aliases={1: 0, 2: 1, 3: 2},
+        scratch_shapes=[pltpu.SemaphoreType.DMA((100,))],
+        compiler_params=pltpu.CompilerParams(vmem_limit_bytes=4 * 1024 * 1024),
+        name="write_rest",
+    )(rest, *(pltpu.with_memory_space_constraint(a, pltpu.HBM) for a in (q, k, v)))
     return q, k, v, n.reshape(8192)
 
 

time: 124 us -> 122 us (0.984)
  Pallas kernels: 123 us -> 121 us
    pallas_call x1, Pallas kernels: 115 us -> 81.4 us  [per_device(): pl.pallas_call(gather_kernel, out_shape=(pltpu.VMEM((16, ROWS, COLS), bf1...]
    pallas_call x1 -> x3, Pallas kernels: 7.49 us -> 39.7 us  [the longest x1 30.1 us: per_device(): pl.pallas_call(rest_kernel, out_shape=pltpu.VMEM((4, LATE, PART, COLS), b...]
where the time goes in v3:
time: 122 us
  Pallas kernels  121 us (99%)
    pallas_call x1, Pallas kernels, per_device(): pl.pallas_call(gather_kernel, out_shape=(pltpu.VMEM((16, ROWS, COLS), bf1...  81.4 us
    pallas_call x1, Pallas kernels, per_device(): pl.pallas_call(rest_kernel, out_shape=pltpu.VMEM((4, LATE, PART, COLS), b...  30.1 us
    pallas_call x1, Pallas kernels, per_device(): pl.pallas_call(write_kernel, out_shape=results + (jax.ShapeDtypeStruct((6...  5.98 us
    pallas_call x1, Pallas kernels, per_device(): pl.pallas_call(write_rest_kernel, out_shape=results, in_specs=[vmem] + [h...  3.63 us

profile of v3, /device:TPU:0, one launch (start us, length us, event | category | flops | bytes accessed | tf_op | source)
XLA Modules:
  0.0 121.7 jit_solution(7874022247333392275)
XLA Ops:
  0.6 81.4 %gather.1 = (bf16[16,1280,512]{2,1,0:T(8,128)(2,1)S(1)}, bf16[64,128]{1,0:T(8,128)(2,1)S(1)}) custom-call(bf16[512,1024]{1,0:T(8,128)(2,1)} %tq.1, bf16[16,512]{1,0:T(8,128)(2,1)} %bitcast.6, bf16[16,1024]{1,0:T(8,128)(2,1)} %hq.1, bf16[512,128]{1,0:T(8,128)(2,1)} %tk.1, bf16[16,512]{1,0:T(8,128)(2,1)} %bitcast.7, bf16[16,128]{1,0:T(8,128)(2,1)} %hk.1, ...), custom_call_target="tpu_custom_call" | custom-call | tf_op jit(solution)/shard_map/gather/pallas_call | solution.py:341
  82.0 6.0 %write.1 = (bf16[1024,8192]{1,0:T(8,128)(2,1)}, bf16[128,8192]{1,0:T(8,128)(2,1)}, bf16[128,8192]{1,0:T(8,128)(2,1)}, bf16[64,128]{1,0:T(8,128)(2,1)}) custom-call(bf16[16,1280,512]{2,1,0:T(8,128)(2,1)S(1)} %get-tuple-element.13.block, bf16[64,128]{1,0:T(8,128)(2,1)S(1)} %get-tuple-element.14.norm), custom_call_target="tpu_custom_call" | custom-call | tf_op jit(solution)/shard_map/write/pallas_call | solution.py:373
  88.0 30.1 %rest.1 = bf16[4,5,320,512]{3,2,1,0:T(8,128)(2,1)S(1)} custom-call(bf16[16,1280,512]{2,1,0:T(8,128)(2,1)S(1)} %get-tuple-element.13.block, bf16[64,128]{1,0:T(8,128)(2,1)} %get-tuple-element.15.norm), custom_call_target="tpu_custom_call" | custom-call | tf_op jit(solution)/shard_map/rest/pallas_call | solution.py:382
  118.1 3.6 %write_rest.1 = (bf16[1024,8192]{1,0:T(8,128)(2,1)}, bf16[128,8192]{1,0:T(8,128)(2,1)}, bf16[128,8192]{1,0:T(8,128)(2,1)}) custom-call(bf16[4,5,320,512]{3,2,1,0:T(8,128)(2,1)S(1)} %rest.1, bf16[1024,8192]{1,0:T(8,128)(2,1)} %get-tuple-element.16.q_in, ...), custom_call_target="tpu_custom_call", output_to_operand_aliasing={{0}: (1, {}), {1}: (2, {}), {2}: (3, {})} | custom-call | tf_op jit(solution)/shard_map/write_rest/pallas_call | solution.py:393

commit v4 on v3

--- a/solution.py
+++ b/solution.py
@@ -38,8 +38,8 @@
 
 
 AHEAD = 4
-BREAK = (10, 13)
-LATE = SLOTS - BREAK[0]
+BREAK = (14, 11)
+LATE = SLOTS - min(BREAK)
 LINKS = schedule()
 ARRIVALS = [
     [(((dy - ty + 1) % 4) - 1, ((dz - tz + 1) % 4) - 1, part) for dy, dz, part in items] for (ty, tz), items in LINKS
@@ -220,7 +220,8 @@
                 send(link, slot).wait_send()
 
     norm_start(0)
-    first, last = BREAK
+    first, last = min(BREAK), max(BREAK)
+    later = core == BREAK.index(last)
     for slot in range(first):
         receive(slot)
         if slot < len(norm_steps):
@@ -230,7 +231,7 @@
         if slot + AHEAD < first:
             launch(slot + AHEAD)
         elif slot + AHEAD < last:
-            pl.when(core == 1)(lambda: launch(slot + AHEAD))
+            pl.when(later)(lambda: launch(slot + AHEAD))
         if slot == len(norm_steps):
             for row in range(64):
                 even = norm_all[row // 4, (row % 4) * 2]
@@ -238,7 +239,7 @@
                 norm_rows[row:row + 1, :] = even + odd
             norm_out[...] = norm_rows[...].astype(jnp.bfloat16)
 
-    @pl.when(core == 1)
+    @pl.when(later)
     def _():
         for slot in range(first, last):
             receive(slot)

time: 122 us -> 117 us (0.959)
  Pallas kernels: 121 us -> 117 us
    pallas_call x1, Pallas kernels: 30.1 us -> 9.24 us  [per_device(): pl.pallas_call(rest_kernel, out_shape=pltpu.VMEM((4, LATE, PART, COLS), b...]
    pallas_call x1, Pallas kernels: 81.4 us -> 97.8 us  [per_device(): pl.pallas_call(gather_kernel, out_shape=(pltpu.VMEM((16, ROWS, COLS), bf1...]
    pallas_call x1, Pallas kernels: 3.63 us -> 1.97 us  [per_device(): pl.pallas_call(write_rest_kernel, out_shape=results, in_specs=[vmem] + [h...]
    pallas_call x1, Pallas kernels: 5.98 us -> 7.55 us  [per_device(): pl.pallas_call(write_kernel, out_shape=results + (jax.ShapeDtypeStruct((6...]
where the time goes in v4:
time: 117 us
  Pallas kernels  117 us (100%)
    pallas_call x1, Pallas kernels, per_device(): pl.pallas_call(gather_kernel, out_shape=(pltpu.VMEM((16, ROWS, COLS), bf1...  97.8 us
    pallas_call x1, Pallas kernels, per_device(): pl.pallas_call(rest_kernel, out_shape=pltpu.VMEM((4, LATE, PART, COLS), b...  9.24 us
    pallas_call x1, Pallas kernels, per_device(): pl.pallas_call(write_kernel, out_shape=results + (jax.ShapeDtypeStruct((6...  7.55 us

profile of v4, /device:TPU:0, one launch (start us, length us, event | category | flops | bytes accessed | tf_op | source)
XLA Modules:
  0.0 117.2 jit_solution(9593586937330600654)
XLA Ops:
  0.6 97.8 %gather.1 = (bf16[16,1280,512]{2,1,0:T(8,128)(2,1)S(1)}, bf16[64,128]{1,0:T(8,128)(2,1)S(1)}) custom-call(bf16[512,1024]{1,0:T(8,128)(2,1)} %tq.1, bf16[16,512]{1,0:T(8,128)(2,1)} %bitcast.6, bf16[16,1024]{1,0:T(8,128)(2,1)} %hq.1, bf16[512,128]{1,0:T(8,128)(2,1)} %tk.1, bf16[16,512]{1,0:T(8,128)(2,1)} %bitcast.7, bf16[16,128]{1,0:T(8,128)(2,1)} %hk.1, ...), custom_call_target="tpu_custom_call" | custom-call | tf_op jit(solution)/shard_map/gather/pallas_call | solution.py:342
  98.5 7.5 %write.1 = (bf16[1024,8192]{1,0:T(8,128)(2,1)}, bf16[128,8192]{1,0:T(8,128)(2,1)}, bf16[128,8192]{1,0:T(8,128)(2,1)}, bf16[64,128]{1,0:T(8,128)(2,1)}) custom-call(bf16[16,1280,512]{2,1,0:T(8,128)(2,1)S(1)} %get-tuple-element.13.block, bf16[64,128]{1,0:T(8,128)(2,1)S(1)} %get-tuple-element.14.norm), custom_call_target="tpu_custom_call" | custom-call | tf_op jit(solution)/shard_map/write/pallas_call | solution.py:374
  106.0 9.2 %rest.1 = bf16[4,4,320,512]{3,2,1,0:T(8,128)(2,1)S(1)} custom-call(bf16[16,1280,512]{2,1,0:T(8,128)(2,1)S(1)} %get-tuple-element.13.block, bf16[64,128]{1,0:T(8,128)(2,1)} %get-tuple-element.15.norm), custom_call_target="tpu_custom_call" | custom-call | tf_op jit(solution)/shard_map/rest/pallas_call | solution.py:383
  115.3 2.0 %write_rest.1 = (bf16[1024,8192]{1,0:T(8,128)(2,1)}, bf16[128,8192]{1,0:T(8,128)(2,1)}, bf16[128,8192]{1,0:T(8,128)(2,1)}) custom-call(bf16[4,4,320,512]{3,2,1,0:T(8,128)(2,1)S(1)} %rest.1, bf16[1024,8192]{1,0:T(8,128)(2,1)} %get-tuple-element.16.q_in, ...), custom_call_target="tpu_custom_call", output_to_operand_aliasing={{0}: (1, {}), {1}: (2, {}), {2}: (3, {})} | custom-call | tf_op jit(solution)/shard_map/write_rest/pallas_call | solution.py:394

commit v5 on v4

--- a/solution.py
+++ b/solution.py
@@ -38,6 +38,7 @@
 
 
 AHEAD = 4
+NORM_AT = {1: 3, 4: 4, 7: 5, 10: 6}
 BREAK = (14, 11)
 LATE = SLOTS - min(BREAK)
 LINKS = schedule()
@@ -94,18 +95,10 @@
         else:
             load(("t", tile), (tk, tv)[tile - 8], t_in.at[tile])
 
+    for tile, _ in TILES[:2]:
+        load_tile(tile)
     load(("l", 0), lq, l_in.at[0])
     load(("h", 0), hq, h_in.at[:, pl.ds(0, 1024)])
-    for tile, _ in TILES[:3]:
-        load_tile(tile)
-    load(("l", 2), lv, l_in.at[2])
-    load(("h", 2), hv, h_in.at[:, pl.ds(1152, TILE)])
-    for tile, _ in TILES[3:7]:
-        load_tile(tile)
-    load(("l", 1), lk, l_in.at[1])
-    load(("h", 1), hk, h_in.at[:, pl.ds(1024, TILE)])
-    for tile, _ in TILES[7:]:
-        load_tile(tile)
     load("nt", nt, nt_in)
     load("ns", ns, ns_in)
 
@@ -114,6 +107,15 @@
         pl.semaphore_signal(barrier, inc=1, device_id={"shard": at(dy, dz)}, device_id_type=MESH)
     for peer in (x * 2 + 1 - core, other(1), other(-1)):
         pl.semaphore_signal(barrier, inc=1, device_id={"tp": peer}, device_id_type=MESH)
+
+    for tile, _ in TILES[2:4]:
+        load_tile(tile)
+    load(("l", 2), lv, l_in.at[2])
+    load(("h", 2), hv, h_in.at[:, pl.ds(1152, TILE)])
+    load(("l", 1), lk, l_in.at[1])
+    load(("h", 1), hk, h_in.at[:, pl.ds(1024, TILE)])
+    for tile, _ in TILES[4:]:
+        load_tile(tile)
 
     def send(link, slot, rows=None):
         (ty, tz), items = LINKS[link]
@@ -121,7 +123,7 @@
         row, count = rows if rows is not None else (part * PART, PART)
         piece = out.at[at(dy, dz), pl.ds(row, count)]
         return pltpu.make_async_remote_copy(
-            src_ref=piece, dst_ref=piece, send_sem=send_sem.at[link, slot], recv_sem=recv_sem.at[link, slot],
+            src_ref=piece, dst_ref=piece, send_sem=send_sem, recv_sem=recv_sem.at[link, slot],
             device_id={"shard": at(ty, tz)}, device_id_type=MESH,
         )
 
@@ -130,7 +132,7 @@
         dy, dz, part = items[slot]
         piece = out.at[at(dy - ty, dz - tz), pl.ds(part * PART, PART)]
         return pltpu.make_async_remote_copy(
-            src_ref=piece, dst_ref=piece, send_sem=send_sem.at[link, slot], recv_sem=recv_sem.at[link, slot],
+            src_ref=piece, dst_ref=piece, send_sem=send_sem, recv_sem=recv_sem.at[link, slot],
             device_id={"shard": at(ty, tz)}, device_id_type=MESH,
         )
 
@@ -159,10 +161,6 @@
         send(link, slot, (row, count)).start()
     for link in (0, 2):
         send(link, 1).start()
-    for slot in range(2, AHEAD):
-        for link in range(4):
-            send(link, slot).start()
-
     loads["nt"].wait()
     loads["ns"].wait()
     gain = nt_in[...] + ns_in[...]
@@ -215,24 +213,28 @@
             arrival(link, slot).wait_recv()
 
     def sent(slots):
-        for slot in slots:
-            for link in range(4):
-                send(link, slot).wait_send()
+        blocks = out.at[pl.ds(0, slots)]
+        pltpu.make_async_copy(blocks, blocks, send_sem).wait()
 
     norm_start(0)
+    for step in range(3):
+        norm_wait(step)
+        norm_start(step + 1)
+    for slot in range(2, AHEAD):
+        launch(slot)
     first, last = min(BREAK), max(BREAK)
     later = core == BREAK.index(last)
     for slot in range(first):
         receive(slot)
-        if slot < len(norm_steps):
-            norm_wait(slot)
-        if slot + 1 < len(norm_steps):
-            norm_start(slot + 1)
+        if slot in NORM_AT:
+            norm_wait(NORM_AT[slot])
+            if NORM_AT[slot] + 1 < len(norm_steps):
+                norm_start(NORM_AT[slot] + 1)
         if slot + AHEAD < first:
             launch(slot + AHEAD)
         elif slot + AHEAD < last:
             pl.when(later)(lambda: launch(slot + AHEAD))
-        if slot == len(norm_steps):
+        if slot == max(NORM_AT):
             for row in range(64):
                 even = norm_all[row // 4, (row % 4) * 2]
                 odd = norm_all[row // 4, (row % 4) * 2 + 1]
@@ -245,9 +247,11 @@
             receive(slot)
             if slot + AHEAD < last:
                 launch(slot + AHEAD)
-        sent(range(first, last))
-
-    sent(range(first))
+        sent(last)
+
+    @pl.when(jnp.logical_not(later))
+    def _():
+        sent(first)
 
 
 def rest_kernel(block, norm, rest, send_sem, recv_sem):
@@ -268,7 +272,7 @@
                 piece = rest.at[from_link, from_slot - first]
             return pltpu.make_async_remote_copy(
                 src_ref=piece, dst_ref=rest.at[link, slot - first],
-                send_sem=send_sem.at[link, slot - first], recv_sem=recv_sem.at[link, slot - first],
+                send_sem=send_sem, recv_sem=recv_sem.at[link, slot - first],
                 device_id={"shard": at(ty, tz)}, device_id_type=MESH,
             )
 
@@ -281,55 +285,52 @@
             if slot + AHEAD < SLOTS:
                 for link in range(4):
                     copy(link, slot + AHEAD).start()
-        for slot in range(first, SLOTS):
-            for link in range(4):
-                copy(link, slot).wait_send()
+        sent = rest.at[:, pl.ds(0, SLOTS - first)]
+        pltpu.make_async_copy(sent, sent, send_sem).wait()
 
     for which in range(2):
         pl.when(core == which)(lambda: run(BREAK[which]))
 
 
-def write_part(copies, sem, src, owner, part, q, k, v):
+def write_part(sem, src, owner, part, q, k, v):
     columns = pl.ds(pl.multiple_of(owner * COLS, COLS), COLS)
     row, count = part * PART, min(PART, 1024 - part * PART)
     pieces = [(0, count, q.at[pl.ds(row, count), columns])]
     if part == D:
         pieces += [(64, 128, k.at[:, columns]), (192, 128, v.at[:, columns])]
     for start, rows, dst in pieces:
-        copies.append(pltpu.make_async_copy(src.at[pl.ds(start, rows)], dst, sem.at[len(copies)]))
-        copies[-1].start()
-
-
-def write_kernel(block, norm, q, k, v, n, sem):
-    shard, core, at = position()
+        pltpu.make_async_copy(src.at[pl.ds(start, rows)], dst, sem).start()
+
+
+def write_kernel(block, norm, q, k, v, n, sem, norm_sem):
+    _, core, at = position()
+    norm_copy = pltpu.make_async_copy(norm, n, norm_sem)
+    norm_copy.start()
 
     def run(first):
-        copies = []
         for part in range(4):
             for far in range(16):
                 dy, dz = far % 4 - 1, far // 4 - 1
                 if PLACE.get((dy, dz, part), (0, -1))[1] < first:
                     src = block.at[at(dy, dz), pl.ds(part * PART, PART)]
-                    write_part(copies, sem, src, at(dy, dz), part, q, k, v)
-        copies.append(pltpu.make_async_copy(norm, n, sem.at[len(copies)]))
-        copies[-1].start()
-        for c in copies:
-            c.wait()
+                    write_part(sem, src, at(dy, dz), part, q, k, v)
+        blocks = block.at[pl.ds(0, 1 + first)]
+        pltpu.make_async_copy(blocks, blocks, sem).wait()
 
     for which in range(2):
         pl.when(core == which)(lambda: run(BREAK[which]))
+    norm_copy.wait()
 
 
 def write_rest_kernel(rest, q_in, k_in, v_in, q, k, v, sem):
     _, core, at = position()
 
     def run(first):
-        copies = []
         for (dy, dz, part), (link, slot) in PLACE.items():
             if slot >= first:
-                write_part(copies, sem, rest.at[link, slot - first], at(dy, dz), part, q, k, v)
-        for c in copies:
-            c.wait()
+                write_part(sem, rest.at[link, slot - first], at(dy, dz), part, q, k, v)
+        parts = rest.at[:, pl.ds(0, SLOTS - first)]
+        pltpu.make_async_copy(parts, parts, sem).wait()
 
     for which in range(2):
         pl.when(core == which)(lambda: run(BREAK[which]))
@@ -353,7 +354,7 @@
             pltpu.VMEM((16, 8, 1, 128), f32),
             pltpu.VMEM((64, 128), f32),
             pltpu.SemaphoreType.DMA((18,)),
-            pltpu.SemaphoreType.DMA((4, SLOTS)),
+            pltpu.SemaphoreType.DMA,
             pltpu.SemaphoreType.DMA((4, SLOTS)),
             pltpu.SemaphoreType.DMA((10,)),
             pltpu.SemaphoreType.DMA((10,)),
@@ -376,7 +377,7 @@
         out_shape=results + (jax.ShapeDtypeStruct((64, 128), bf16),),
         in_specs=[vmem, vmem],
         out_specs=(hbm,) * 4,
-        scratch_shapes=[pltpu.SemaphoreType.DMA((100,))],
+        scratch_shapes=[pltpu.SemaphoreType.DMA, pltpu.SemaphoreType.DMA],
         compiler_params=pltpu.CompilerParams(vmem_limit_bytes=4 * 1024 * 1024),
         name="write",
     )(block, norm)
@@ -385,7 +386,7 @@
         out_shape=pltpu.VMEM((4, LATE, PART, COLS), bf16),
         in_specs=[vmem, hbm],
         out_specs=vmem,
-        scratch_shapes=[pltpu.SemaphoreType.DMA((4, LATE)), pltpu.SemaphoreType.DMA((4, LATE))],
+        scratch_shapes=[pltpu.SemaphoreType.DMA, pltpu.SemaphoreType.DMA((4, LATE))],
         compiler_params=pltpu.CompilerParams(
             collective_id=1, has_side_effects=True, vmem_limit_bytes=4 * 1024 * 1024
         ),
@@ -397,7 +398,7 @@
         in_specs=[vmem] + [hbm] * 3,
         out_specs=(hbm,) * 3,
         input_output_aliases={1: 0, 2: 1, 3: 2},
-        scratch_shapes=[pltpu.SemaphoreType.DMA((100,))],
+        scratch_shapes=[pltpu.SemaphoreType.DMA],
         compiler_params=pltpu.CompilerParams(vmem_limit_bytes=4 * 1024 * 1024),
         name="write_rest",
     )(rest, *(pltpu.with_memory_space_constraint(a, pltpu.HBM) for a in (q, k, v)))

time: 117 us -> 116 us (level)
  Pallas kernels: 117 us -> 115 us
where the time goes in v5:
time: 116 us
  Pallas kernels  115 us (99%)
    pallas_call x1, Pallas kernels, per_device(): pl.pallas_call(gather_kernel, out_shape=(pltpu.VMEM((16, ROWS, COLS), bf1...  98.4 us
    pallas_call x1, Pallas kernels, per_device(): pl.pallas_call(rest_kernel, out_shape=pltpu.VMEM((4, LATE, PART, COLS), b...  9.21 us
    pallas_call x1, Pallas kernels, per_device(): pl.pallas_call(write_kernel, out_shape=results + (jax.ShapeDtypeStruct((6...  6.67 us

profile of v5, /device:TPU:0, one launch (start us, length us, event | category | flops | bytes accessed | tf_op | source)
XLA Modules:
  0.0 116.0 jit_solution(14366927591604939239)
XLA Ops:
  0.6 98.4 %gather.1 = (bf16[16,1280,512]{2,1,0:T(8,128)(2,1)S(1)}, bf16[64,128]{1,0:T(8,128)(2,1)S(1)}) custom-call(bf16[512,1024]{1,0:T(8,128)(2,1)} %tq.1, bf16[16,512]{1,0:T(8,128)(2,1)} %bitcast.6, bf16[16,1024]{1,0:T(8,128)(2,1)} %hq.1, bf16[512,128]{1,0:T(8,128)(2,1)} %tk.1, bf16[16,512]{1,0:T(8,128)(2,1)} %bitcast.7, bf16[16,128]{1,0:T(8,128)(2,1)} %hk.1, ...), custom_call_target="tpu_custom_call" | custom-call | tf_op jit(solution)/shard_map/gather/pallas_call | solution.py:343
  99.1 6.7 %write.1 = (bf16[1024,8192]{1,0:T(8,128)(2,1)}, bf16[128,8192]{1,0:T(8,128)(2,1)}, bf16[128,8192]{1,0:T(8,128)(2,1)}, bf16[64,128]{1,0:T(8,128)(2,1)}) custom-call(bf16[16,1280,512]{2,1,0:T(8,128)(2,1)S(1)} %get-tuple-element.13.block, bf16[64,128]{1,0:T(8,128)(2,1)S(1)} %get-tuple-element.14.norm), custom_call_target="tpu_custom_call" | custom-call | tf_op jit(solution)/shard_map/write/pallas_call | solution.py:375
  105.7 9.2 %rest.1 = bf16[4,4,320,512]{3,2,1,0:T(8,128)(2,1)S(1)} custom-call(bf16[16,1280,512]{2,1,0:T(8,128)(2,1)S(1)} %get-tuple-element.13.block, bf16[64,128]{1,0:T(8,128)(2,1)} %get-tuple-element.15.norm), custom_call_target="tpu_custom_call" | custom-call | tf_op jit(solution)/shard_map/rest/pallas_call | solution.py:384
  115.0 1.1 write_rest.1

commit v6 on v5

--- a/solution.py
+++ b/solution.py
@@ -74,7 +74,7 @@
     tq, lq, hq, tk, lk, hk, tv, lv, hv, nt, ns,
     out, norm_out,
     t_in, l_in, h_in, nt_in, ns_in, norm_all, norm_rows,
-    load_sem, send_sem, recv_sem, norm_send, norm_recv,
+    load_sem, send_sem, recv_sem, norm_send, norm_recv, ready,
 ):
     shard, core, at = position()
     tp = lax.axis_index("tp")
@@ -102,11 +102,19 @@
     load("nt", nt, nt_in)
     load("ns", ns, ns_in)
 
+    y = shard % 4
+    peers = [{"shard": at(dy, dz)} for (dy, dz), _ in LINKS]
+    peers += [{"tp": x * 2 + 1 - core}, {"tp": other(1)}, {"tp": other(-1)}]
+    mirror = (1, 0, 3, 2, 4, 6, 5)
+    later = (y < 3, y == 0, z < 3, z == 0, core == 1, x < 3, x == 0)
     barrier = pltpu.get_barrier_semaphore()
-    for (dy, dz), _ in LINKS:
-        pl.semaphore_signal(barrier, inc=1, device_id={"shard": at(dy, dz)}, device_id_type=MESH)
-    for peer in (x * 2 + 1 - core, other(1), other(-1)):
-        pl.semaphore_signal(barrier, inc=1, device_id={"tp": peer}, device_id_type=MESH)
+    earlier_ones = 7
+    for who, peer in enumerate(peers):
+        earlier_ones = earlier_ones - later[who].astype(jnp.int32)
+
+        @pl.when(later[who])
+        def _():
+            pl.semaphore_signal(barrier, inc=1, device_id=peer, device_id_type=MESH)
 
     for tile, _ in TILES[2:4]:
         load_tile(tile)
@@ -116,6 +124,18 @@
     load(("h", 1), hk, h_in.at[:, pl.ds(1024, TILE)])
     for tile, _ in TILES[4:]:
         load_tile(tile)
+
+    pl.when(earlier_ones > 0)(lambda: pl.semaphore_wait(barrier, earlier_ones))
+    for who, peer in enumerate(peers):
+
+        @pl.when(jnp.logical_not(later[who]))
+        def _():
+            pl.semaphore_signal(ready.at[mirror[who]], inc=1, device_id=peer, device_id_type=MESH)
+
+    def greet(who):
+        @pl.when(later[who])
+        def _():
+            pl.semaphore_wait(ready.at[who], 1)
 
     def send(link, slot, rows=None):
         (ty, tz), items = LINKS[link]
@@ -149,24 +169,36 @@
         whole = t_in[tile].astype(jnp.float32).T + mix_rate * product
         out[shard, tile * TILE:(tile + 1) * TILE, :] = whole.astype(jnp.bfloat16)
 
+    def send_pieces(pieces):
+        for link, slot, row, count in pieces:
+            pl.when(jnp.logical_not(later[link]))(lambda: send(link, slot, (row, count)).start())
+
     waiting = ()
-    for place, (tile, pieces) in enumerate(TILES):
+    for tile, pieces in TILES:
         merge(tile)
-        if place == 1:
-            pl.semaphore_wait(barrier, 7)
-        for link, slot, row, count in waiting:
-            send(link, slot, (row, count)).start()
+        send_pieces(waiting)
         waiting = pieces
-    for link, slot, row, count in waiting:
-        send(link, slot, (row, count)).start()
-    for link in (0, 2):
-        send(link, 1).start()
+
     loads["nt"].wait()
     loads["ns"].wait()
     gain = nt_in[...] + ns_in[...]
     both = jnp.concatenate([gain, gain], axis=1)
     half = lax.broadcasted_iota(jnp.int32, (1, 128), 1) // 64
     norm_all[shard, tp] = jnp.where(half == core, both, 0.0)
+
+    send_pieces(waiting)
+    for link in (0, 2):
+        pl.when(jnp.logical_not(later[link]))(lambda: send(link, 1).start())
+    for link in (0, 2, 1, 3):
+
+        @pl.when(later[link])
+        def _():
+            pl.semaphore_wait(ready.at[link], 1)
+            send(link, 0).start()
+            send(link, 1).start()
+
+    for who in (4, 5, 6):
+        greet(who)
 
     def norm_copy(step, piece, peer):
         return pltpu.make_async_remote_copy(
@@ -223,7 +255,7 @@
     for slot in range(2, AHEAD):
         launch(slot)
     first, last = min(BREAK), max(BREAK)
-    later = core == BREAK.index(last)
+    breaks_late = core == BREAK.index(last)
     for slot in range(first):
         receive(slot)
         if slot in NORM_AT:
@@ -233,7 +265,7 @@
         if slot + AHEAD < first:
             launch(slot + AHEAD)
         elif slot + AHEAD < last:
-            pl.when(later)(lambda: launch(slot + AHEAD))
+            pl.when(breaks_late)(lambda: launch(slot + AHEAD))
         if slot == max(NORM_AT):
             for row in range(64):
                 even = norm_all[row // 4, (row % 4) * 2]
@@ -241,7 +273,7 @@
                 norm_rows[row:row + 1, :] = even + odd
             norm_out[...] = norm_rows[...].astype(jnp.bfloat16)
 
-    @pl.when(later)
+    @pl.when(breaks_late)
     def _():
         for slot in range(first, last):
             receive(slot)
@@ -249,17 +281,30 @@
                 launch(slot + AHEAD)
         sent(last)
 
-    @pl.when(jnp.logical_not(later))
+    @pl.when(jnp.logical_not(breaks_late))
     def _():
         sent(first)
 
 
-def rest_kernel(block, norm, rest, send_sem, recv_sem):
-    _, core, at = position()
+def rest_kernel(block, norm, rest, send_sem, recv_sem, ready):
+    shard, core, at = position()
+    z, y = shard // 4, shard % 4
+    later = (y < 3, y == 0, z < 3, z == 0)
     barrier = pltpu.get_barrier_semaphore()
-    for (dy, dz), _ in LINKS:
-        pl.semaphore_signal(barrier, inc=1, device_id={"shard": at(dy, dz)}, device_id_type=MESH)
-    pl.semaphore_wait(barrier, 4)
+    earlier_ones = 4
+    for link, ((dy, dz), _) in enumerate(LINKS):
+        earlier_ones = earlier_ones - later[link].astype(jnp.int32)
+
+        @pl.when(later[link])
+        def _():
+            pl.semaphore_signal(barrier, inc=1, device_id={"shard": at(dy, dz)}, device_id_type=MESH)
+
+    pl.when(earlier_ones > 0)(lambda: pl.semaphore_wait(barrier, earlier_ones))
+    for link, ((dy, dz), _) in enumerate(LINKS):
+
+        @pl.when(jnp.logical_not(later[link]))
+        def _():
+            pl.semaphore_signal(ready.at[link ^ 1], inc=1, device_id={"shard": at(dy, dz)}, device_id_type=MESH)
 
     def run(first):
         def copy(link, slot):
@@ -276,15 +321,22 @@
                 device_id={"shard": at(ty, tz)}, device_id_type=MESH,
             )
 
-        for slot in range(first, min(first + AHEAD, SLOTS)):
-            for link in range(4):
+        def launch(link):
+            for slot in range(first, SLOTS):
                 copy(link, slot).start()
+
+        for link in range(4):
+            pl.when(jnp.logical_not(later[link]))(lambda: launch(link))
+        for link in (0, 2, 1, 3):
+
+            @pl.when(later[link])
+            def _():
+                pl.semaphore_wait(ready.at[link], 1)
+                launch(link)
+
         for slot in range(first, SLOTS):
             for link in range(4):
                 copy(link, slot).wait_recv()
-            if slot + AHEAD < SLOTS:
-                for link in range(4):
-                    copy(link, slot + AHEAD).start()
         sent = rest.at[:, pl.ds(0, SLOTS - first)]
         pltpu.make_async_copy(sent, sent, send_sem).wait()
 
@@ -358,6 +410,7 @@
             pltpu.SemaphoreType.DMA((4, SLOTS)),
             pltpu.SemaphoreType.DMA((10,)),
             pltpu.SemaphoreType.DMA((10,)),
+            pltpu.SemaphoreType.REGULAR((7,)),
         ],
         compiler_params=pltpu.CompilerParams(
             collective_id=0, has_side_effects=True, vmem_limit_bytes=12 * 1024 * 1024
@@ -386,7 +439,9 @@
         out_shape=pltpu.VMEM((4, LATE, PART, COLS), bf16),
         in_specs=[vmem, hbm],
         out_specs=vmem,
-        scratch_shapes=[pltpu.SemaphoreType.DMA, pltpu.SemaphoreType.DMA((4, LATE))],
+        scratch_shapes=[
+            pltpu.SemaphoreType.DMA, pltpu.SemaphoreType.DMA((4, LATE)), pltpu.SemaphoreType.REGULAR((4,))
+        ],
         compiler_params=pltpu.CompilerParams(
             collective_id=1, has_side_effects=True, vmem_limit_bytes=4 * 1024 * 1024
         ),

time: 116 us -> 114 us (0.983)
    pallas_call x1, Pallas kernels: 98.4 us -> 96.7 us  [per_device(): pl.pallas_call(gather_kernel, out_shape=(pltpu.VMEM((16, ROWS, COLS), bf1...]
where the time goes in v6:
time: 114 us
  Pallas kernels  114 us (100%)
    pallas_call x1, Pallas kernels, per_device(): pl.pallas_call(gather_kernel, out_shape=(pltpu.VMEM((16, ROWS, COLS), bf1...  96.7 us
    pallas_call x1, Pallas kernels, per_device(): pl.pallas_call(rest_kernel, out_shape=pltpu.VMEM((4, LATE, PART, COLS), b...  9.22 us
    pallas_call x1, Pallas kernels, per_device(): pl.pallas_call(write_kernel, out_shape=results + (jax.ShapeDtypeStruct((6...  6.67 us

profile of v6, /device:TPU:0, one launch (start us, length us, event | category | flops | bytes accessed | tf_op | source)
XLA Modules:
  0.0 114.3 jit_solution(6702791067405235841)
XLA Ops:
  0.6 96.7 %gather.1 = (bf16[16,1280,512]{2,1,0:T(8,128)(2,1)S(1)}, bf16[64,128]{1,0:T(8,128)(2,1)S(1)}) custom-call(bf16[512,1024]{1,0:T(8,128)(2,1)} %tq.1, bf16[16,512]{1,0:T(8,128)(2,1)} %bitcast.6, bf16[16,1024]{1,0:T(8,128)(2,1)} %hq.1, bf16[512,128]{1,0:T(8,128)(2,1)} %tk.1, bf16[16,512]{1,0:T(8,128)(2,1)} %bitcast.7, bf16[16,128]{1,0:T(8,128)(2,1)} %hk.1, ...), custom_call_target="tpu_custom_call" | custom-call | tf_op jit(solution)/shard_map/gather/pallas_call | solution.py:395
  97.3 6.7 %write.1 = (bf16[1024,8192]{1,0:T(8,128)(2,1)}, bf16[128,8192]{1,0:T(8,128)(2,1)}, bf16[128,8192]{1,0:T(8,128)(2,1)}, bf16[64,128]{1,0:T(8,128)(2,1)}) custom-call(bf16[16,1280,512]{2,1,0:T(8,128)(2,1)S(1)} %get-tuple-element.13.block, bf16[64,128]{1,0:T(8,128)(2,1)S(1)} %get-tuple-element.14.norm), custom_call_target="tpu_custom_call" | custom-call | tf_op jit(solution)/shard_map/write/pallas_call | solution.py:428
  104.0 9.2 %rest.1 = bf16[4,4,320,512]{3,2,1,0:T(8,128)(2,1)S(1)} custom-call(bf16[16,1280,512]{2,1,0:T(8,128)(2,1)S(1)} %get-tuple-element.13.block, bf16[64,128]{1,0:T(8,128)(2,1)} %get-tuple-element.15.norm), custom_call_target="tpu_custom_call" | custom-call | tf_op jit(solution)/shard_map/rest/pallas_call | solution.py:437
  113.3 1.1 write_rest.1

commit v7 on v6

--- a/solution.py
+++ b/solution.py
@@ -42,6 +42,7 @@
 BREAK = (14, 11)
 LATE = SLOTS - min(BREAK)
 LINKS = schedule()
+SHORT, SHIFT = (2, 4), 48
 ARRIVALS = [
     [(((dy - ty + 1) % 4) - 1, ((dz - tz + 1) % 4) - 1, part) for dy, dz, part in items] for (ty, tz), items in LINKS
 ]
@@ -74,7 +75,7 @@
     tq, lq, hq, tk, lk, hk, tv, lv, hv, nt, ns,
     out, norm_out,
     t_in, l_in, h_in, nt_in, ns_in, norm_all, norm_rows,
-    load_sem, send_sem, recv_sem, norm_send, norm_recv, ready,
+    load_sem, send_sem, recv_sem, norm_send, norm_recv, ready, shift_sem,
 ):
     shard, core, at = position()
     tp = lax.axis_index("tp")
@@ -137,23 +138,32 @@
         def _():
             pl.semaphore_wait(ready.at[who], 1)
 
+    def copy(link, slot, owner, rows):
+        piece = out.at[owner, pl.ds(*rows)]
+        (dy, dz), _ = LINKS[link]
+        leaves = send_sem.at[2 if (link, slot) == SHORT else (0, 0, 1, 0)[link]]
+        return pltpu.make_async_remote_copy(
+            src_ref=piece, dst_ref=piece, send_sem=leaves, recv_sem=recv_sem.at[link, slot],
+            device_id={"shard": at(dy, dz)}, device_id_type=MESH,
+        )
+
     def send(link, slot, rows=None):
+        dy, dz, part = LINKS[link][1][slot]
+        return copy(link, slot, at(dy, dz), rows if rows is not None else (part * PART, PART))
+
+    def arrival(link, slot, cut=0):
         (ty, tz), items = LINKS[link]
         dy, dz, part = items[slot]
-        row, count = rows if rows is not None else (part * PART, PART)
-        piece = out.at[at(dy, dz), pl.ds(row, count)]
+        return copy(link, slot, at(dy - ty, dz - tz), (part * PART, PART - cut))
+
+    part = LINKS[SHORT[0]][1][SHORT[1]][2]
+    cut_rows, shifted_rows = (part * PART, PART - SHIFT), (part * PART + PART - SHIFT, SHIFT)
+
+    def shifted(dz):
+        piece = out.at[at(0, dz), pl.ds(*shifted_rows)]
         return pltpu.make_async_remote_copy(
-            src_ref=piece, dst_ref=piece, send_sem=send_sem, recv_sem=recv_sem.at[link, slot],
-            device_id={"shard": at(ty, tz)}, device_id_type=MESH,
-        )
-
-    def arrival(link, slot):
-        (ty, tz), items = LINKS[link]
-        dy, dz, part = items[slot]
-        piece = out.at[at(dy - ty, dz - tz), pl.ds(part * PART, PART)]
-        return pltpu.make_async_remote_copy(
-            src_ref=piece, dst_ref=piece, send_sem=send_sem, recv_sem=recv_sem.at[link, slot],
-            device_id={"shard": at(ty, tz)}, device_id_type=MESH,
+            src_ref=piece, dst_ref=piece, send_sem=shift_sem.at[0], recv_sem=shift_sem.at[1],
+            device_id={"shard": at(0, -1)}, device_id_type=MESH,
         )
 
     def merge(tile):
@@ -238,15 +248,28 @@
 
     def launch(slot):
         for link in range(4):
-            send(link, slot).start()
+            if (link, slot) == SHORT:
+                pl.when(z == 3)(lambda: send(link, slot, cut_rows).start())
+                pl.when(z != 3)(lambda: send(link, slot).start())
+            else:
+                send(link, slot).start()
 
     def receive(slot):
         for link in range(4):
-            arrival(link, slot).wait_recv()
+            if (link, slot) == SHORT:
+                pl.when(z == 0)(lambda: arrival(link, slot, SHIFT).wait_recv())
+                pl.when(z != 0)(lambda: arrival(link, slot).wait_recv())
+            else:
+                arrival(link, slot).wait_recv()
 
     def sent(slots):
-        blocks = out.at[pl.ds(0, slots)]
-        pltpu.make_async_copy(blocks, blocks, send_sem).wait()
+        for leaves, parts in (
+            (0, out.at[pl.ds(0, slots), pl.ds(0, 3 * PART)]), (1, out.at[pl.ds(0, slots - 1), pl.ds(0, PART)])
+        ):
+            pltpu.make_async_copy(parts, parts, send_sem.at[leaves]).wait()
+        pl.when(z == 3)(lambda: send(*SHORT, cut_rows).wait_send())
+        pl.when(z != 3)(lambda: send(*SHORT).wait_send())
+        pl.when(z == 1)(lambda: shifted(1).wait_send())
 
     norm_start(0)
     for step in range(3):
@@ -262,6 +285,10 @@
             norm_wait(NORM_AT[slot])
             if NORM_AT[slot] + 1 < len(norm_steps):
                 norm_start(NORM_AT[slot] + 1)
+        if slot == 1:
+            pl.when(z == 1)(lambda: shifted(1).start())
+        if slot == 6:
+            pl.when(z == 0)(lambda: shifted(2).wait_recv())
         if slot + AHEAD < first:
             launch(slot + AHEAD)
         elif slot + AHEAD < last:
@@ -406,11 +433,12 @@
             pltpu.VMEM((16, 8, 1, 128), f32),
             pltpu.VMEM((64, 128), f32),
             pltpu.SemaphoreType.DMA((18,)),
-            pltpu.SemaphoreType.DMA,
+            pltpu.SemaphoreType.DMA((3,)),
             pltpu.SemaphoreType.DMA((4, SLOTS)),
             pltpu.SemaphoreType.DMA((10,)),
             pltpu.SemaphoreType.DMA((10,)),
             pltpu.SemaphoreType.REGULAR((7,)),
+            pltpu.SemaphoreType.DMA((2,)),
         ],
         compiler_params=pltpu.CompilerParams(
             collective_id=0, has_side_effects=True, vmem_limit_bytes=12 * 1024 * 1024

time: 114 us -> 114 us (level)
  no operation moved by 1% of the time
where the time goes in v7:
time: 114 us
  Pallas kernels  113 us (99%)
    pallas_call x1, Pallas kernels, per_device(): pl.pallas_call(gather_kernel, out_shape=(pltpu.VMEM((16, ROWS, COLS), bf1...  96.1 us
    pallas_call x1, Pallas kernels, per_device(): pl.pallas_call(rest_kernel, out_shape=pltpu.VMEM((4, LATE, PART, COLS), b...  9.03 us
    pallas_call x1, Pallas kernels, per_device(): pl.pallas_call(write_kernel, out_shape=results + (jax.ShapeDtypeStruct((6...  6.67 us

profile of v7, /device:TPU:0, one launch (start us, length us, event | category | flops | bytes accessed | tf_op | source)
XLA Modules:
  0.0 113.6 jit_solution(17058786036107965471)
XLA Ops:
  0.6 96.1 %gather.1 = (bf16[16,1280,512]{2,1,0:T(8,128)(2,1)S(1)}, bf16[64,128]{1,0:T(8,128)(2,1)S(1)}) custom-call(bf16[512,1024]{1,0:T(8,128)(2,1)} %tq.1, bf16[16,512]{1,0:T(8,128)(2,1)} %bitcast.6, bf16[16,1024]{1,0:T(8,128)(2,1)} %hq.1, bf16[512,128]{1,0:T(8,128)(2,1)} %tk.1, bf16[16,512]{1,0:T(8,128)(2,1)} %bitcast.7, bf16[16,128]{1,0:T(8,128)(2,1)} %hk.1, ...), custom_call_target="tpu_custom_call" | custom-call | tf_op jit(solution)/shard_map/gather/pallas_call | solution.py:422
  96.8 6.7 %write.1 = (bf16[1024,8192]{1,0:T(8,128)(2,1)}, bf16[128,8192]{1,0:T(8,128)(2,1)}, bf16[128,8192]{1,0:T(8,128)(2,1)}, bf16[64,128]{1,0:T(8,128)(2,1)}) custom-call(bf16[16,1280,512]{2,1,0:T(8,128)(2,1)S(1)} %get-tuple-element.13.block, bf16[64,128]{1,0:T(8,128)(2,1)S(1)} %get-tuple-element.14.norm), custom_call_target="tpu_custom_call" | custom-call | tf_op jit(solution)/shard_map/write/pallas_call | solution.py:456
  103.4 9.0 %rest.1 = bf16[4,4,320,512]{3,2,1,0:T(8,128)(2,1)S(1)} custom-call(bf16[16,1280,512]{2,1,0:T(8,128)(2,1)S(1)} %get-tuple-element.13.block, bf16[64,128]{1,0:T(8,128)(2,1)} %get-tuple-element.15.norm), custom_call_target="tpu_custom_call" | custom-call | tf_op jit(solution)/shard_map/rest/pallas_call | solution.py:465
  112.5 1.1 write_rest.1

commit v8 on v7

--- a/solution.py
+++ b/solution.py
@@ -371,10 +371,11 @@
         pl.when(core == which)(lambda: run(BREAK[which]))
 
 
-def write_part(sem, src, owner, part, q, k, v):
+def write_part(sem, src, owner, part, q, k, v, cuts=1):
     columns = pl.ds(pl.multiple_of(owner * COLS, COLS), COLS)
     row, count = part * PART, min(PART, 1024 - part * PART)
-    pieces = [(0, count, q.at[pl.ds(row, count), columns])]
+    step = count // cuts
+    pieces = [(at, step, q.at[pl.ds(row + at, step), columns]) for at in range(0, count, step)]
     if part == D:
         pieces += [(64, 128, k.at[:, columns]), (192, 128, v.at[:, columns])]
     for start, rows, dst in pieces:
@@ -407,7 +408,7 @@
     def run(first):
         for (dy, dz, part), (link, slot) in PLACE.items():
             if slot >= first:
-                write_part(sem, rest.at[link, slot - first], at(dy, dz), part, q, k, v)
+                write_part(sem, rest.at[link, slot - first], at(dy, dz), part, q, k, v, 4 if slot >= max(BREAK) else 1)
         parts = rest.at[:, pl.ds(0, SLOTS - first)]
         pltpu.make_async_copy(parts, parts, sem).wait()
 

time: 114 us -> 114 us (level)
  no operation moved by 1% of the time
where the time goes in v8:
time: 114 us
  Pallas kernels  113 us (99%)
    pallas_call x1, Pallas kernels, per_device(): pl.pallas_call(gather_kernel, out_shape=(pltpu.VMEM((16, ROWS, COLS), bf1...  96.1 us
    pallas_call x1, Pallas kernels, per_device(): pl.pallas_call(rest_kernel, out_shape=pltpu.VMEM((4, LATE, PART, COLS), b...  9.03 us
    pallas_call x1, Pallas kernels, per_device(): pl.pallas_call(write_kernel, out_shape=results + (jax.ShapeDtypeStruct((6...  6.67 us

profile of v8, /device:TPU:0, one launch (start us, length us, event | category | flops | bytes accessed | tf_op | source)
XLA Modules:
  0.0 113.6 jit_solution(590084893907032893)
XLA Ops:
  0.6 96.1 %gather.1 = (bf16[16,1280,512]{2,1,0:T(8,128)(2,1)S(1)}, bf16[64,128]{1,0:T(8,128)(2,1)S(1)}) custom-call(bf16[512,1024]{1,0:T(8,128)(2,1)} %tq.1, bf16[16,512]{1,0:T(8,128)(2,1)} %bitcast.6, bf16[16,1024]{1,0:T(8,128)(2,1)} %hq.1, bf16[512,128]{1,0:T(8,128)(2,1)} %tk.1, bf16[16,512]{1,0:T(8,128)(2,1)} %bitcast.7, bf16[16,128]{1,0:T(8,128)(2,1)} %hk.1, ...), custom_call_target="tpu_custom_call" | custom-call | tf_op jit(solution)/shard_map/gather/pallas_call | solution.py:423
  96.8 6.7 %write.1 = (bf16[1024,8192]{1,0:T(8,128)(2,1)}, bf16[128,8192]{1,0:T(8,128)(2,1)}, bf16[128,8192]{1,0:T(8,128)(2,1)}, bf16[64,128]{1,0:T(8,128)(2,1)}) custom-call(bf16[16,1280,512]{2,1,0:T(8,128)(2,1)S(1)} %get-tuple-element.13.block, bf16[64,128]{1,0:T(8,128)(2,1)S(1)} %get-tuple-element.14.norm), custom_call_target="tpu_custom_call" | custom-call | tf_op jit(solution)/shard_map/write/pallas_call | solution.py:457
  103.4 9.0 %rest.1 = bf16[4,4,320,512]{3,2,1,0:T(8,128)(2,1)S(1)} custom-call(bf16[16,1280,512]{2,1,0:T(8,128)(2,1)S(1)} %get-tuple-element.13.block, bf16[64,128]{1,0:T(8,128)(2,1)} %get-tuple-element.15.norm), custom_call_target="tpu_custom_call" | custom-call | tf_op jit(solution)/shard_map/rest/pallas_call | solution.py:466
  112.5 1.1 write_rest.1
